TPU v7x, 32 devices: a whole 2x2x4 slice. The times are simulated.
32 devices in a mesh: row: 4 (over y, core), col: 8 (over z, x).
Axes of the slice: x: 2, y: 2, z: 4, core: 2. Of those that a mesh axis runs over, the one named last changes fastest.
Arguments:
- tokens: bfloat16 [40, 8192], P('col', 'row'), may hold values from -6 to 6
- grad_out: bfloat16 [40, 8192], P('col', 'row'), may hold values from -6 to 6
- gate_weight: bfloat16 [8192, 28672], P('row', 'col'), may hold values from -0.0625 to 0.0625
- up_weight: bfloat16 [8192, 28672], P('row', 'col'), may hold values from -0.0625 to 0.0625
- down_weight: bfloat16 [28672, 8192], P('col', 'row'), may hold values from -0.03125 to 0.03125
Outputs:
- grad_tokens: bfloat16 [40, 8192], P('col', 'row')
- grad_gate_weight: bfloat16 [8192, 28672], P('row', 'col')
- grad_up_weight: bfloat16 [8192, 28672], P('row', 'col')
- grad_down_weight: bfloat16 [28672, 8192], P('col', 'row')
All inputs are finite; a program needn't handle non-finite values.
Results may differ from a plain program's by a relative error of at most 0.0049.
Values may be sent and summed in bfloat16 or wider, within the bound.
A program may use at most 192 MiB of HBM per device.

v0:
```python
import jax
import jax.numpy as jnp
from jax import lax
from jax.sharding import PartitionSpec as P


def hidden_grads(gate_sum, up_sum, back_sum):
    sigmoid_gate = 1.0 / (1.0 + jnp.exp(-gate_sum))
    activated = gate_sum * sigmoid_gate
    hidden = (activated * up_sum).astype(jnp.bfloat16)
    grad_up = (back_sum * activated).astype(jnp.bfloat16)
    slope = sigmoid_gate * (1.0 + gate_sum * (1.0 - sigmoid_gate))
    grad_gate = (back_sum * up_sum * slope).astype(jnp.bfloat16)
    return (hidden, grad_gate, grad_up)


def shards(tokens, grad_out, gate_weight, up_weight, down_weight):
    tok_full, grad_full = (
        lax.all_gather(tokens, "col", axis=0, tiled=True),
        lax.all_gather(grad_out, "col", axis=0, tiled=True),
    )
    hidden_width = gate_weight.shape[1]
    gate_part = jnp.dot(tok_full, gate_weight, preferred_element_type=jnp.float32)
    up_part = jnp.dot(tok_full, up_weight, preferred_element_type=jnp.float32)
    back_part = jnp.einsum("td,fd->tf", grad_full, down_weight, preferred_element_type=jnp.float32)
    sums = lax.psum(jnp.concatenate([gate_part, up_part, back_part], axis=1), "row")
    hidden, grad_gate, grad_up = hidden_grads(
        sums[:, :hidden_width],
        sums[:, hidden_width : 2 * hidden_width],
        sums[:, 2 * hidden_width :],
    )
    grad_down_weight = jnp.einsum(
        "tf,td->fd", hidden, grad_full, preferred_element_type=jnp.float32
    ).astype(jnp.bfloat16)
    grad_gate_weight = jnp.einsum(
        "td,tf->df", tok_full, grad_gate, preferred_element_type=jnp.float32
    ).astype(jnp.bfloat16)
    grad_up_weight = jnp.einsum(
        "td,tf->df", tok_full, grad_up, preferred_element_type=jnp.float32
    ).astype(jnp.bfloat16)
    total = jnp.einsum("tf,df->td", grad_gate, gate_weight, preferred_element_type=jnp.float32)
    grad_tokens = lax.psum_scatter(
        total + jnp.einsum("tf,df->td", grad_up, up_weight, preferred_element_type=jnp.float32),
        "col",
        scatter_dimension=0,
        tiled=True,
    ).astype(jnp.bfloat16)
    return (grad_tokens, grad_gate_weight, grad_up_weight, grad_down_weight)


def solution(mesh):
    placed = (P("col", "row"), P("col", "row"), P("row", "col"), P("row", "col"), P("col", "row"))
    return jax.shard_map(
        shards,
        mesh=mesh,
        in_specs=placed,
        out_specs=(P("col", "row"), P("row", "col"), P("row", "col"), P("col", "row")),
        check_vma=False,
    )
```

profile of v0, /device:TPU:0, one launch (start us, length us, event | category | flops | bytes accessed | tf_op | source)
XLA Modules:
  0.0 270.7 jit_solution(15416068624223160820)
XLA Ops:
  7.2 0.0 all-reduce.4.cloned.1.call-start
  7.2 32.8 %all-gather = bf16[8,5,2048]{2,1,0:T(8,128)(2,1)S(1)} all-gather(bf16[1,5,2048]{2,1,0:T(8,128)(2,1)} %bitcast.22), channel_id=1, replica_groups=mesh['row'=4,'col'=8] {'col'}, dimensions={0}, use_global_device_ids=true | all-gather | bytes 184320 | tf_op jit(solution)/shard_map/all_gather | solution.py:19
  40.0 0.1 reshape.9
  40.1 0.0 copy-start
  40.1 7.9 %fusion.5 = f32[40,3584]{1,0:T(8,128)S(1)} fusion(bf16[40,2048]{1,0:T(8,128)(2,1)S(1)} %reshape.9, bf16[2048,3584]{1,0:T(8,128)(2,1)} %param.7), kind=kOutput, calls=%fused_computation.14 | convolution fusion | flops 587202560 | bytes 15417344 | tf_op jit(solution)/shard_map/dot_general | solution.py:23
  48.0 1.5 copy-done
  49.4 0.0 copy-start.1
  49.4 2.6 fusion.6
  52.0 0.0 copy-start.2
  52.0 0.0 copy-done.1
  52.0 30.9 %all-gather.1 = bf16[8,5,2048]{2,1,0:T(8,128)(2,1)S(1)} all-gather(bf16[1,5,2048]{2,1,0:T(8,128)(2,1)S(1)} %bitcast.23), channel_id=1, replica_groups=mesh['row'=4,'col'=8] {'col'}, dimensions={0}, use_global_device_ids=true | all-gather | bytes 184320 | tf_op jit(solution)/shard_map/all_gather | solution.py:20
  82.9 0.1 reshape.11
  83.0 9.6 %fusion.7 = f32[40,3584]{1,0:T(8,128)S(1)} fusion(bf16[40,2048]{1,0:T(8,128)(2,1)S(1)} %reshape.11, bf16[3584,2048]{1,0:T(8,128)(2,1)} %param.9), kind=kOutput, calls=%fused_computation.16 | convolution fusion | flops 587202560 | bytes 15417344 | tf_op jit(solution)/shard_map/td,fd->tf/dot_general | solution.py:25
  92.6 1.3 pad_maximum_fusion
  93.9 0.0 all-reduce.4.cloned.1.call-update
  94.0 0.0 copy-done.2
  94.0 0.6 dynamic-slice
  95.2 45.3 %all-reduce.4.cloned.1.call-done = f32[40,10752]{1,0:T(8,128)} async-done(((f32[40,10752]{1,0:T(8,128)}), f32[40,10752]{1,0:T(8,128)}) %all-reduce.4.cloned.1.call-update) | async-done | bytes 1720336 | tf_op jit(solution)/shard_map/psum | solution.py:26
  140.5 1.7 multiply_convert_fusion.1
  142.2 9.5 %fusion.8 = f32[40,2048]{1,0:T(8,128)S(1)} fusion(bf16[40,3584]{1,0:T(8,128)(2,1)S(1)} %get-tuple-element.17, bf16[2048,3584]{1,0:T(8,128)(2,1)} %param.7), kind=kOutput, calls=%fused_computation.17 | convolution fusion | flops 587202560 | bytes 15294464 | tf_op jit(solution)/shard_map/tf,df->td/dot_general | solution.py:41
  151.7 7.6 %fusion = bf16[2048,3584]{0,1:T(8,128)(2,1)} fusion(bf16[40,3584]{1,0:T(8,128)(2,1)S(1)} %get-tuple-element.17, bf16[40,2048]{1,0:T(8,128)(2,1)S(1)} %reshape.9), kind=kOutput, calls=%fused_computation.3 | convolution fusion | flops 594542592 | bytes 15130624 | tf_op jit(solution)/shard_map/td,tf->df/dot_general | solution.py:35
  159.3 7.3 %fusion.1 = bf16[2048,3584]{0,1:T(8,128)(2,1)} fusion(bf16[40,3584]{1,0:T(8,128)(2,1)S(1)} %get-tuple-element.16, bf16[40,2048]{1,0:T(8,128)(2,1)S(1)} %reshape.9), kind=kOutput, calls=%fused_computation.4 | convolution fusion | flops 594542592 | bytes 15130624 | tf_op jit(solution)/shard_map/td,tf->df/dot_general | solution.py:38
  166.6 9.5 %convolution_add_fusion = f32[40,2048]{1,0:T(8,128)S(1)} fusion(f32[40,2048]{1,0:T(8,128)S(1)} %fusion.8, bf16[40,3584]{1,0:T(8,128)(2,1)S(1)} %get-tuple-element.16, bf16[2048,3584]{1,0:T(8,128)(2,1)} %param.8), kind=kOutput, calls=%fused_computation.5 | convolution fusion | flops 587284480 | bytes 15622144 | tf_op jit(solution)/shard_map/tf,df->td/dot_general | solution.py:43
  176.2 41.0 %all-reduce.5 = bf16[40,2048]{1,0:T(8,128)(2,1)S(1)} all-reduce(f32[40,2048]{1,0:T(8,128)S(1)} %convolution_add_fusion), channel_id=2, replica_groups=mesh['row'=4,'col'=8] {'col'}, use_global_device_ids=true, to_apply=%region_1.0.clone | all-reduce | flops 81920 | bytes 491520
  217.1 18.6 %copy.13 = bf16[2048,3584]{1,0:T(8,128)(2,1)} copy(bf16[2048,3584]{0,1:T(8,128)(2,1)} %fusion) | data formatting | bytes 29360128
  235.8 18.6 %copy.14 = bf16[2048,3584]{1,0:T(8,128)(2,1)} copy(bf16[2048,3584]{0,1:T(8,128)(2,1)} %fusion.1) | data formatting | bytes 29360128
  254.4 0.6 dynamic-slice_convert_fusion
  255.0 8.8 %convolution_convert_fusion = bf16[3584,2048]{1,0:T(8,128)(2,1)} fusion(bf16[40,2048]{1,0:T(8,128)(2,1)S(1)} %reshape.11, f32[40,10752]{1,0:T(8,128)} %all-reduce.4.cloned.1.call-done), kind=kOutput, calls=%fused_computation | convolution fusion | flops 595402752 | bytes 15990784 | tf_op jit(solution)/shard_map/tf,td->fd/dot_general | solution.py:32
Async XLA Ops:
  7.2 133.3 %all-reduce.4.cloned.1.call-start = ((), (), s32[]{:S(2)}) async-start(), calls=%async_computation | async-start | bytes 3440640 | tf_op jit(solution)/shard_map/psum | solution.py:26
  40.1 9.4 %copy-start = (bf16[2048,3584]{1,0:T(8,128)(2,1)S(1)}, bf16[2048,3584]{1,0:T(8,128)(2,1)}, u32[]{:S(2)}) copy-start(bf16[2048,3584]{1,0:T(8,128)(2,1)} %param.8) | copy-start | bytes 44040196
  49.4 2.6 copy-start.1
  52.0 42.0 %copy-start.2 = (u32[32]{0:T(128)S(1)}, u32[32]{0:T(128)}, u32[]{:S(2)}) copy-start(u32[32]{0:T(128)} %constant.6) | copy-start | bytes 388
Sparse Core Ops, SparseCore 0:
  94.1 46.3 all-reduce.3
where the time goes:
time: 272 us; the launch traced here: 271 us
  blocking collectives  105 us (39%)
  matrix products  62.9 us (23%)
  waiting for transfers between devices  45.3 us (17%)
  local copies, waits for them, and re-layouts  40.1 us (15%)
  between operations  14.8 us (5%)
  other arithmetic  2.98 us (1%)
    psum x1, waiting for transfers between devices, shards(): lax.psum(jnp.concatenate([gate_part, up_part, back_part], axis=1), 'row')  45.3 us
    unnamed x1, blocking collectives  41 us
    unnamed x11, local copies, waits for them, and re-layouts  39.5 us
    all_gather x1, blocking collectives, shards(): lax.all_gather(tokens, 'col', axis=0, tiled=True)  32.8 us
    all_gather x1, blocking collectives, shards(): lax.all_gather(grad_out, 'col', axis=0, tiled=True)  30.9 us
    dot_general x1, matrix products, shards(): jnp.einsum('td,fd->tf', grad_full, down_weight, preferred_element_type=jn...  9.61 us
    dot_general x1, matrix products, shards(): jnp.einsum('tf,df->td', grad_up, up_weight, preferred_element_type=jnp.fl...  9.53 us
    dot_general x1, matrix products, shards(): jnp.einsum('tf,df->td', grad_gate, gate_weight, preferred_element_type=jn...  9.51 us
  transfers between devices with their start and end apart: 1, of which 1 were waited for; matrix products, arithmetic and copies ran while one was open for 0% of the time, Pallas kernels for 0%

commit v1 on v0

v1 whole, which is shorter than its diff:
```python
import functools

import jax
import jax.numpy as jnp
from jax import lax
from jax.experimental import pallas as pl
from jax.experimental.pallas import tpu as pltpu
from jax.sharding import PartitionSpec as P

F32 = jnp.float32
BF16 = jnp.bfloat16
LAST = (((1,), (1,)), ((), ()))
MESH = pl.DeviceIdType.MESH


def hidden_grads(gate_sum, up_sum, back_sum):
    sigmoid_gate = 1.0 / (1.0 + jnp.exp(-gate_sum))
    activated = gate_sum * sigmoid_gate
    hidden = (activated * up_sum).astype(BF16)
    grad_up = (back_sum * activated).astype(BF16)
    slope = sigmoid_gate * (1.0 + gate_sum * (1.0 - sigmoid_gate))
    grad_gate = (back_sum * up_sum * slope).astype(BF16)
    return (hidden, grad_gate, grad_up)


def exchange_kernel(
    rows, cols, tok_in, grad_in, gate_hbm, up_hbm, down_hbm,
    tok_out, grad_out, acts_out, dtok_out,
    gate_buf, up_buf, down_buf, tok_slots, grad_slots, stage, tok_all, grad_all,
    part_send, part_recv, acts, acc, dtok_send, dtok_recv,
    load_sem, own_sem, tok_ssem, tok_rsem, part_ssem, part_rsem,
    acts_ssem, acts_rsem, fwd_ssem, fwd_rsem, dtok_ssem, dtok_rsem, out_sem,
):
    row, col = lax.axis_index("row"), lax.axis_index("col")
    chips = rows // 2
    chip, core = row // 2, row % 2
    width = gate_buf.shape[2]
    few = tok_in.shape[0]

    def peer(dy, dc):
        return ((chip + dy) % chips) * 2 + (core + dc) % 2

    offsets = [(dy, dc) for dy in range(1, chips) for dc in (0, 1)] + [(0, 1), (0, 0)]

    loads = []
    for o, (dy, dc) in enumerate(offsets):
        at = pl.multiple_of(peer(dy, dc) * width, 128)
        trio = (
            pltpu.make_async_copy(gate_hbm.at[:, pl.ds(at, width)], gate_buf.at[o], load_sem.at[0, o]),
            pltpu.make_async_copy(up_hbm.at[:, pl.ds(at, width)], up_buf.at[o], load_sem.at[1, o]),
            pltpu.make_async_copy(down_hbm.at[pl.ds(at, width), :], down_buf.at[o], load_sem.at[2, o]),
        )
        loads.append(trio)
    for load in loads[0]:
        load.start()

    barrier = pltpu.get_barrier_semaphore()
    for dy, dc in offsets[:-1]:
        pl.semaphore_signal(barrier, inc=1, device_id=(peer(dy, dc), col), device_id_type=MESH)
    for s in range(1, cols):
        pl.semaphore_signal(barrier, inc=1, device_id=(row, (col + s) % cols), device_id_type=MESH)
    own_tok = pltpu.make_async_copy(tok_in, tok_slots.at[col], own_sem.at[0])
    own_grad = pltpu.make_async_copy(grad_in, grad_slots.at[col], own_sem.at[1])
    own_tok.start()
    own_grad.start()
    pl.semaphore_wait(barrier, rows - 1 + cols - 1)

    def gather(s, slot):
        to = (row, (col + s) % cols)
        return [
            pltpu.make_async_remote_copy(
                src_ref=src, dst_ref=dst.at[slot], send_sem=tok_ssem.at[a, s], recv_sem=tok_rsem.at[a, s],
                device_id=to, device_id_type=MESH,
            )
            for a, (src, dst) in enumerate(((tok_in, tok_slots), (grad_in, grad_slots)))
        ]

    for s in range(1, cols):
        for copy in gather(s, col):
            copy.start()
    for trio in loads[1:]:
        for load in trio:
            load.start()
    own_tok.wait()
    own_grad.wait()
    for s in range(1, cols):
        for copy in gather(s, (col + cols - s) % cols):
            copy.wait_recv()
    for slots, whole in ((tok_slots, tok_all), (grad_slots, grad_all)):
        for k in range(cols):
            stage[k * few : (k + 1) * few, :] = slots[k].astype(F32)
        whole[...] = stage[...].astype(BF16)
    outs = [
        pltpu.make_async_copy(tok_all, tok_out, out_sem.at[0]),
        pltpu.make_async_copy(grad_all, grad_out, out_sem.at[1]),
    ]
    for copy in outs:
        copy.start()

    def partial(o):
        for load in loads[o]:
            load.wait()
        gate_part = jnp.dot(tok_all[...], gate_buf[o], preferred_element_type=F32)
        up_part = jnp.dot(tok_all[...], up_buf[o], preferred_element_type=F32)
        back_part = lax.dot_general(down_buf[o], grad_all[...], LAST, preferred_element_type=F32).T
        return gate_part, up_part, back_part

    sends = []
    for o, (dy, dc) in enumerate(offsets[:-1]):
        for i, part in enumerate(partial(o)):
            part_send[o, i] = part.astype(BF16)
        copy = pltpu.make_async_remote_copy(
            src_ref=part_send.at[o], dst_ref=part_recv.at[o],
            send_sem=part_ssem.at[o], recv_sem=part_rsem.at[o],
            device_id=(peer(dy, dc), col), device_id_type=MESH,
        )
        copy.start()
        sends.append(copy)
    last = rows - 1
    sums = list(partial(last))
    for o in range(rows - 1):
        sends[o].wait_recv()
        sums = [total + part_recv[o, i].astype(F32) for i, total in enumerate(sums)]
    for i, value in enumerate(hidden_grads(*sums)):
        acts[row, i] = value

    def share(sems, n, q, to):
        return pltpu.make_async_remote_copy(
            src_ref=acts.at[q], dst_ref=acts.at[q], send_sem=sems[0].at[n], recv_sem=sems[1].at[n],
            device_id=(to, col), device_id_type=MESH,
        )

    direct, forward = (acts_ssem, acts_rsem), (fwd_ssem, fwd_rsem)
    other = peer(0, 1)
    for dy in range(1, chips):
        share(direct, dy, row, peer(dy, 0)).start()
    share(forward, 0, row, other).start()

    block = acc.shape[0] // 4

    def add_block(o, q, first):
        @pl.loop(0, 4)
        def _(t):
            at = pl.ds(pl.multiple_of(t * block, block), block)
            value = lax.dot_general(gate_buf[o, at, :], acts[q, 1], LAST, preferred_element_type=F32)
            value += lax.dot_general(up_buf[o, at, :], acts[q, 2], LAST, preferred_element_type=F32)
            acc[at, :] = value if first else acc[at, :] + value

    add_block(last, row, True)
    share(forward, 0, other, other).wait_recv()
    add_block(last - 1, other, False)
    for dy in range(1, chips):
        q = peer(chips - dy, 0)
        share(direct, dy, q, peer(dy, 0)).wait_recv()
        share(forward, dy, q, other).start()
        add_block(2 * (chips - dy - 1), q, False)
    for dy in range(1, chips):
        q = peer(chips - dy, 1)
        share(forward, dy, q, other).wait_recv()
        add_block(2 * (chips - dy - 1) + 1, q, False)

    total = acc[...].T
    stage[...] = total
    for k in range(cols):
        dtok_send[k] = stage[k * few : (k + 1) * few, :].astype(BF16)

    def scatter(s):
        to = (col + s) % cols
        return pltpu.make_async_remote_copy(
            src_ref=dtok_send.at[to], dst_ref=dtok_recv.at[s], send_sem=dtok_ssem.at[s],
            recv_sem=dtok_rsem.at[s], device_id=(row, to), device_id_type=MESH,
        )

    for s in range(1, cols):
        scatter(s).start()
    outs.append(pltpu.make_async_copy(acts, acts_out, out_sem.at[2]))
    outs[-1].start()
    result = dtok_send[col].astype(F32)
    for s in range(1, cols):
        scatter(s).wait_recv()
        result += dtok_recv[s].astype(F32)
    dtok_out[...] = result.astype(BF16)

    for copy in outs:
        copy.wait()
    for s in range(1, cols):
        for copy in gather(s, col):
            copy.wait_send()
        scatter(s).wait_send()
    for copy in sends:
        copy.wait_send()
    share(forward, 0, row, other).wait_send()
    for dy in range(1, chips):
        share(direct, dy, row, peer(dy, 0)).wait_send()
        share(forward, dy, peer(chips - dy, 0), other).wait_send()


def exchange(rows, cols, tokens, grad_out, gate_weight, up_weight, down_weight):
    few, depth = tokens.shape
    hidden = gate_weight.shape[1]
    width = hidden // rows
    many = few * cols
    dma = pltpu.SemaphoreType.DMA
    any_spec = pl.BlockSpec(memory_space=pl.ANY)
    vmem_spec = pl.BlockSpec(memory_space=pltpu.VMEM)
    shape = jax.ShapeDtypeStruct
    return pl.pallas_call(
        functools.partial(exchange_kernel, rows, cols),
        out_shape=(
            shape((many, depth), BF16),
            shape((many, depth), BF16),
            shape((rows, 3, many, width), BF16),
            shape((few, depth), BF16),
        ),
        in_specs=[vmem_spec, vmem_spec, any_spec, any_spec, any_spec],
        out_specs=(any_spec, any_spec, any_spec, vmem_spec),
        scratch_shapes=[
            pltpu.VMEM((rows, depth, width), BF16),
            pltpu.VMEM((rows, depth, width), BF16),
            pltpu.VMEM((rows, width, depth), BF16),
            pltpu.VMEM((cols, few, depth), BF16),
            pltpu.VMEM((cols, few, depth), BF16),
            pltpu.VMEM((many, depth), F32),
            pltpu.VMEM((many, depth), BF16),
            pltpu.VMEM((many, depth), BF16),
            pltpu.VMEM((rows - 1, 3, many, width), BF16),
            pltpu.VMEM((rows - 1, 3, many, width), BF16),
            pltpu.VMEM((rows, 3, many, width), BF16),
            pltpu.VMEM((depth, many), F32),
            pltpu.VMEM((cols, few, depth), BF16),
            pltpu.VMEM((cols, few, depth), BF16),
            dma((3, rows)),
            dma((2,)),
            dma((2, cols)),
            dma((2, cols)),
            dma((rows,)),
            dma((rows,)),
            dma((rows,)),
            dma((rows,)),
            dma((rows,)),
            dma((rows,)),
            dma((cols,)),
            dma((cols,)),
            dma((3,)),
        ],
        compiler_params=pltpu.CompilerParams(
            collective_id=0, has_side_effects=True, vmem_limit_bytes=62 * 1024 * 1024
        ),
        name="exchange",
    )(tokens, grad_out, gate_weight, up_weight, down_weight)


def outer_kernel(tok, grad, acts, gate_out, up_out, down_out, hidden_t):
    rows, _, _, width = acts.shape

    @pl.when(pl.program_id(0) == 0)
    def _():
        for q in range(rows):
            hidden_t[q * width : (q + 1) * width, :] = acts[q, 0].astype(F32).T.astype(BF16)

    tok_t = tok[...].astype(F32).T.astype(BF16)
    for out, i in ((gate_out, 1), (up_out, 2)):
        @pl.loop(0, rows)
        def _(q):
            at = pl.ds(pl.multiple_of(q * width, 128), width)
            out[:, at] = jnp.dot(tok_t, acts[q, i], preferred_element_type=F32).astype(BF16)

    @pl.loop(0, 2 * rows)
    def _(t):
        at = pl.ds(pl.multiple_of(t * (width // 2), 64), width // 2)
        down_out[at, :] = jnp.dot(hidden_t[at, :], grad[...], preferred_element_type=F32).astype(BF16)


def outer(tok, grad, acts):
    many, depth = tok.shape
    rows, _, _, width = acts.shape
    hidden = rows * width
    steps = 8
    while depth % (steps * 128):
        steps //= 2
    part = depth // steps
    shape = jax.ShapeDtypeStruct
    return pl.pallas_call(
        outer_kernel,
        grid=(steps,),
        out_shape=(
            shape((depth, hidden), BF16),
            shape((depth, hidden), BF16),
            shape((hidden, depth), BF16),
        ),
        in_specs=[
            pl.BlockSpec((many, part), lambda i: (0, i)),
            pl.BlockSpec((many, part), lambda i: (0, i)),
            pl.BlockSpec((rows, 3, many, width), lambda i: (0, 0, 0, 0)),
        ],
        out_specs=(
            pl.BlockSpec((part, hidden), lambda i: (i, 0)),
            pl.BlockSpec((part, hidden), lambda i: (i, 0)),
            pl.BlockSpec((hidden, part), lambda i: (0, i)),
        ),
        scratch_shapes=[pltpu.VMEM((hidden, many), BF16)],
        compiler_params=pltpu.CompilerParams(
            dimension_semantics=("arbitrary",), vmem_limit_bytes=40 * 1024 * 1024
        ),
        name="outer",
    )(tok, grad, acts)


def shards(rows, cols, tokens, grad_out, gate_weight, up_weight, down_weight):
    tok, grad, acts, grad_tokens = exchange(
        rows, cols, tokens, grad_out, gate_weight, up_weight, down_weight
    )
    return (grad_tokens, *outer(tok, grad, acts))


def plain_shards(tokens, grad_out, gate_weight, up_weight, down_weight):
    tok_full, grad_full = (
        lax.all_gather(tokens, "col", axis=0, tiled=True),
        lax.all_gather(grad_out, "col", axis=0, tiled=True),
    )
    hidden_width = gate_weight.shape[1]
    gate_part = jnp.dot(tok_full, gate_weight, preferred_element_type=F32)
    up_part = jnp.dot(tok_full, up_weight, preferred_element_type=F32)
    back_part = jnp.einsum("td,fd->tf", grad_full, down_weight, preferred_element_type=F32)
    sums = lax.psum(jnp.concatenate([gate_part, up_part, back_part], axis=1), "row")
    hidden, grad_gate, grad_up = hidden_grads(*jnp.split(sums, 3, axis=1))
    grad_down_weight = jnp.einsum("tf,td->fd", hidden, grad_full, preferred_element_type=F32).astype(BF16)
    grad_gate_weight = jnp.einsum("td,tf->df", tok_full, grad_gate, preferred_element_type=F32).astype(BF16)
    grad_up_weight = jnp.einsum("td,tf->df", tok_full, grad_up, preferred_element_type=F32).astype(BF16)
    total = jnp.einsum("tf,df->td", grad_gate, gate_weight, preferred_element_type=F32)
    total += jnp.einsum("tf,df->td", grad_up, up_weight, preferred_element_type=F32)
    grad_tokens = lax.psum_scatter(total, "col", scatter_dimension=0, tiled=True).astype(BF16)
    return (grad_tokens, grad_gate_weight, grad_up_weight, grad_down_weight)


def choose(rows, cols, *operands):
    depth, hidden = operands[2].shape
    if hidden % (rows * 128) or depth % 128 or rows % 2:
        return plain_shards(*operands)
    return shards(rows, cols, *operands)


def solution(mesh):
    placed = (P("col", "row"), P("col", "row"), P("row", "col"), P("row", "col"), P("col", "row"))
    return jax.shard_map(
        functools.partial(choose, mesh.shape["row"], mesh.shape["col"]),
        mesh=mesh,
        in_specs=placed,
        out_specs=(P("col", "row"), P("row", "col"), P("row", "col"), P("col", "row")),
        check_vma=False,
    )
```

time: 272 us -> 88.2 us (0.32)
  blocking collectives: 105 us -> 0 us
  Pallas kernels: 0 us -> 82.9 us
  matrix products: 62.9 us -> 0 us
  waiting for transfers between devices: 45.3 us -> 0 us
  local copies, waits for them, and re-layouts: 40.1 us -> 4.36 us
  between operations: 14.8 us -> 0.65 us
  other arithmetic: 2.98 us -> 0 us
    pallas_call x0 -> x2, Pallas kernels: none -> 82.9 us  [the longest x1 50.7 us: exchange(): pl.pallas_call(functools.partial(exchange_kernel, rows, cols), out_shape=...]
    all_gather x2 -> x0, blocking collectives: 63.7 us -> none  [the longest x1 32.8 us: shards(): lax.all_gather(tokens, 'col', axis=0, tiled=True)]
    dot_general x8 -> x0, matrix products: 62.9 us -> none  [the longest x1 9.61 us: shards(): jnp.einsum('td,fd->tf', grad_full, down_weight, preferred_element_type=jn...]
    psum x1 -> x0, waiting for transfers between devices: 45.3 us -> none  [shards(): lax.psum(jnp.concatenate([gate_part, up_part, back_part], axis=1), 'row')]
    unnamed x1 -> x0, blocking collectives: 41 us -> none
    unnamed x11 -> x7, local copies, waits for them, and re-layouts: 39.5 us -> 4.36 us
  transfers between devices with their start and end apart: 1 -> 0, of which waited for: 1 -> 0; matrix products, arithmetic and copies ran while one was open for 0% -> 0% of each run, Pallas kernels for 0% -> 0%
where the time goes in v1:
time: 88.2 us; the launch traced here: 87.9 us
  Pallas kernels  82.9 us (94%)
  local copies, waits for them, and re-layouts  4.36 us (5%)
    pallas_call x1, Pallas kernels, exchange(): pl.pallas_call(functools.partial(exchange_kernel, rows, cols), out_shape=...  50.7 us
    pallas_call x1, Pallas kernels, outer(): pl.pallas_call(outer_kernel, grid=(steps,), out_shape=(shape((depth, hidd...  32.2 us
    unnamed x7, local copies, waits for them, and re-layouts  4.36 us

profile of v1, /device:TPU:0, one launch (start us, length us, event | category | flops | bytes accessed | tf_op | source)
XLA Modules:
  0.0 87.9 jit_solution(17353706237036347008)
XLA Ops:
  0.6 50.7 %exchange.1 = (bf16[40,2048]{1,0:T(8,128)(2,1)}, bf16[40,2048]{1,0:T(8,128)(2,1)}, bf16[4,3,40,896]{3,2,1,0:T(8,128)(2,1)}, bf16[5,2048]{1,0:T(8,128)(2,1)}) custom-call(bf16[5,2048]{1,0:T(8,128)(2,1)} %tok_in.1, bf16[5,2048]{1,0:T(8,128)(2,1)} %grad_in.1, bf16[2048,3584]{1,0:T(8,128)(2,1)} %gate_hbm.1, bf16[2048,3584]{1,0:T(8,128)(2,1)} %up_hbm.1, ...), custom_call_target="tpu_custom_call" | custom-call | tf_op jit(solution)/shard_map/exchange/pallas_call | solution.py:207
  51.3 0.0 copy-start
  51.3 1.1 %copy-done = bf16[4,3,40,896]{3,2,1,0:T(8,128)(2,1)S(1)} copy-done((bf16[4,3,40,896]{3,2,1,0:T(8,128)(2,1)S(1)}, bf16[4,3,40,896]{3,2,1,0:T(8,128)(2,1)}, u32[]{:S(2)}) %copy-start) | copy-done | bytes 860184
  52.5 0.0 copy-start.1
  52.5 0.9 %copy-done.1 = bf16[40,2048]{1,0:T(8,128)(2,1)S(1)} copy-done((bf16[40,2048]{1,0:T(8,128)(2,1)S(1)}, bf16[40,2048]{1,0:T(8,128)(2,1)}, u32[]{:S(2)}) %copy-start.1) | copy-done | bytes 163864
  53.4 0.0 copy-start.2
  53.4 0.9 %copy-done.2 = bf16[40,2048]{1,0:T(8,128)(2,1)S(1)} copy-done((bf16[40,2048]{1,0:T(8,128)(2,1)S(1)}, bf16[40,2048]{1,0:T(8,128)(2,1)}, u32[]{:S(2)}) %copy-start.2) | copy-done | bytes 163864
  54.3 32.2 %outer.1 = (bf16[2048,3584]{1,0:T(8,128)(2,1)}, bf16[2048,3584]{1,0:T(8,128)(2,1)}, bf16[3584,2048]{1,0:T(8,128)(2,1)}) custom-call(bf16[40,2048]{1,0:T(8,128)(2,1)S(1)} %copy-done.1, bf16[40,2048]{1,0:T(8,128)(2,1)S(1)} %copy-done.2, bf16[4,3,40,896]{3,2,1,0:T(8,128)(2,1)S(1)} %copy-done), custom_call_target="tpu_custom_call" | custom-call | tf_op jit(solution)/shard_map/outer/pallas_call | solution.py:283
  86.5 1.4 %copy.10 = bf16[5,2048]{1,0:T(8,128)(2,1)} copy(bf16[5,2048]{1,0:T(8,128)(2,1)} %get-tuple-element.22) | data formatting | bytes 40960
Async XLA Ops:
  51.3 1.2 %copy-start = (bf16[4,3,40,896]{3,2,1,0:T(8,128)(2,1)S(1)}, bf16[4,3,40,896]{3,2,1,0:T(8,128)(2,1)}, u32[]{:S(2)}) copy-start(bf16[4,3,40,896]{3,2,1,0:T(8,128)(2,1)} %get-tuple-element.14.acts) | copy-start | bytes 2580484
  52.5 0.9 %copy-start.1 = (bf16[40,2048]{1,0:T(8,128)(2,1)S(1)}, bf16[40,2048]{1,0:T(8,128)(2,1)}, u32[]{:S(2)}) copy-start(bf16[40,2048]{1,0:T(8,128)(2,1)} %get-tuple-element.12.tok) | copy-start | bytes 491524
  53.4 0.9 %copy-start.2 = (bf16[40,2048]{1,0:T(8,128)(2,1)S(1)}, bf16[40,2048]{1,0:T(8,128)(2,1)}, u32[]{:S(2)}) copy-start(bf16[40,2048]{1,0:T(8,128)(2,1)} %get-tuple-element.13.grad) | copy-start | bytes 491524
